TPU v7x, 32 devices: a whole 2x2x4 slice. The times are simulated.
32 devices in a mesh: dp: 8 (over z, y), head: 4 (over x, core).
Axes of the slice: x: 2, y: 2, z: 4, core: 2. Of those that a mesh axis runs over, the one named last changes fastest.
Arguments:
- tokens: bfloat16 [8, 6312, 768], P('dp', 'head'), may hold values from -6 to 6
- frames: int32 [8], P('dp'), may hold values from 4 to 16
- text_mask: int32 [8, 40], P('dp'), may hold values 0 or 1
- latents: bfloat16 [8, 128, 768], P('dp'), may hold values from -6 to 6
- cross_q: bfloat16 [768, 768], P('head'), may hold values from -0.21875 to 0.21875
- cross_kv: bfloat16 [2, 768, 768], P(None, 'head'), may hold values from -0.21875 to 0.21875
- cross_out: bfloat16 [768, 768], P('head'), may hold values from -3.5 to 3.5
- cross_up: bfloat16 [768, 3072], P(None, 'head'), may hold values from -0.21875 to 0.21875
- cross_down: bfloat16 [3072, 768], P('head'), may hold values from -0.109375 to 0.109375
- self_qkv: bfloat16 [3, 768, 768], P(None, 'head'), may hold values from -0.21875 to 0.21875
- self_out: bfloat16 [768, 768], P('head'), may hold values from -0.875 to 0.875
- self_up: bfloat16 [768, 3072], P(None, 'head'), may hold values from -0.21875 to 0.21875
- self_down: bfloat16 [3072, 768], P('head'), may hold values from -0.109375 to 0.109375
- head_bias: float32 [2, 2, 768], P(None, None, 'head'), may hold values from -1.8 to 1.8
- up_bias: float32 [2, 3072], P(None, 'head'), may hold values from -1.8 to 1.8
- out_bias: float32 [2, 2, 768], replicated, may hold values from -1.8 to 1.8
- norm_gain: float32 [5, 768], replicated, may hold values from 0.5 to 1.5
- norm_bias: float32 [5, 768], replicated, may hold values from -1.8 to 1.8
- latents_cot: float32 [8, 128, 768], P('dp'), may hold values from -6 to 6
Outputs:
- latents_out: float32 [8, 128, 768], P('dp')
- grad_tokens: bfloat16 [8, 6312, 768], P('dp', 'head')
- grad_latents: float32 [8, 128, 768], P('dp')
- grad_cross_q: float32 [768, 768], P('head', 'dp')
- grad_cross_kv: float32 [2, 768, 768], P(None, 'head', 'dp')
- grad_cross_out: float32 [768, 768], P('head', 'dp')
- grad_cross_up: float32 [768, 3072], P('dp', 'head')
- grad_cross_down: float32 [3072, 768], P('head', 'dp')
- grad_self_qkv: float32 [3, 768, 768], P(None, 'head', 'dp')
- grad_self_out: float32 [768, 768], P('head', 'dp')
- grad_self_up: float32 [768, 3072], P('dp', 'head')
- grad_self_down: float32 [3072, 768], P('head', 'dp')
- grad_head_bias: float32 [2, 2, 768], P(None, None, 'head')
- grad_up_bias: float32 [2, 3072], P(None, 'head')
- grad_out_bias: float32 [2, 2, 768], P(None, None, 'head')
- grad_norm_gain: float32 [5, 768], P(None, 'head')
- grad_norm_bias: float32 [5, 768], P(None, 'head')
Inputs may be any that keep to these rules, and one draw needn't show every extreme that they name: The patches of frames at or after frames[c] are padding.
All inputs are finite; a program needn't handle non-finite values. No bound on the sum of `text_mask` on one device may be relied on, other than what follows from the above.
Results may differ from a plain program's by a relative error of at most 0.018.
Values may be sent and summed in bfloat16 or wider, within the bound.
A program may use at most 128 MiB of HBM per device.

v0:
```python
from functools import partial
import jax
import jax.numpy as jnp
from jax import lax
from jax.sharding import PartitionSpec as P

HD = 64
P_SIZE = 392
F_MAX = 16
EPSILON = 1e-05
NEGATIVE = -1e30


def normed(tensor, gain_row, shift_row):
    row_mean = jnp.mean(tensor, axis=-1, keepdims=True)
    centered = tensor - row_mean
    spread = jnp.mean(centered * centered, axis=-1, keepdims=True)
    return centered * lax.rsqrt(spread + EPSILON) * gain_row + shift_row


def share_of(tensor, head_index, head_width):
    return lax.dynamic_slice_in_dim(tensor, head_index * head_width, head_width, tensor.ndim - 1)


def split_heads(tensor, heads_here):
    return tensor.reshape(
        tensor.shape[0], tensor.shape[1], heads_here, tensor.shape[2] // heads_here
    )


def merge_heads(tensor):
    return tensor.reshape(tensor.shape[0], tensor.shape[1], tensor.shape[2] * tensor.shape[3])


def join_heads(partial_sum):
    return lax.psum(partial_sum.astype(jnp.bfloat16), "head").astype(jnp.float32)


def join_back(partial_sum):
    return lax.psum(partial_sum.astype(jnp.bfloat16), "head").astype(jnp.float32)


def scores_of(queries, key_rows, usable):
    scores = jnp.einsum("qhe,khe->hqk", queries, key_rows, preferred_element_type=jnp.float32)
    return jnp.where(usable[None, None, :], scores, NEGATIVE)


def attend_parts(parts):
    queries, key_rows, values, usable = parts
    scores = scores_of(queries, key_rows, usable)
    row_max = jnp.max(scores, axis=-1, keepdims=True)
    powers = jnp.exp(scores - row_max)
    totals = jnp.sum(powers, axis=-1, keepdims=True)
    chances = (powers / totals).astype(jnp.bfloat16)
    mixture = jnp.einsum("hqk,khe->qhe", chances, values, preferred_element_type=jnp.float32)
    return (mixture.astype(jnp.bfloat16), row_max, totals)


def back_parts(parts):
    queries, key_rows, values, usable, row_max, totals, grad_mix = parts
    scores = scores_of(queries, key_rows, usable)
    chances = jnp.exp(scores - row_max) / totals
    rounded = chances.astype(jnp.bfloat16)
    grad_values = jnp.einsum(
        "hqk,qhe->khe", rounded, grad_mix, preferred_element_type=jnp.float32
    ).astype(jnp.bfloat16)
    grad_chances = jnp.einsum("qhe,khe->hqk", grad_mix, values, preferred_element_type=jnp.float32)
    inner_sum = jnp.sum(chances * grad_chances, axis=-1, keepdims=True)
    grad_scores = (chances * (grad_chances - inner_sum)).astype(jnp.bfloat16)
    grad_queries = jnp.einsum(
        "hqk,khe->qhe", grad_scores, key_rows, preferred_element_type=jnp.float32
    ).astype(jnp.bfloat16)
    grad_keys = jnp.einsum(
        "hqk,qhe->khe", grad_scores, queries, preferred_element_type=jnp.float32
    ).astype(jnp.bfloat16)
    return (grad_queries, grad_keys, grad_values)


def feed_forward(tensor, gain_row, shift_row, weight_up, bias_up, weight_down):
    hidden = normed(tensor, gain_row, shift_row).astype(jnp.bfloat16)
    pre_act = (
        jnp.einsum("cnd,df->cnf", hidden, weight_up, preferred_element_type=jnp.float32) + bias_up
    )
    activation = jax.nn.gelu(pre_act, approximate=True).astype(jnp.bfloat16)
    partial_sum = jnp.einsum(
        "cnf,fd->cnd", activation, weight_down, preferred_element_type=jnp.float32
    )
    return (join_heads(partial_sum), (hidden, pre_act, activation))


def feed_back(tensor, gain_row, shift_row, weight_up, weight_down, saved_acts, grad_out):
    hidden, pre_act, activation = saved_acts
    grad_branch = grad_out.astype(jnp.bfloat16)
    grad_weight_down = jnp.einsum(
        "cnf,cnd->fd", activation, grad_branch, preferred_element_type=jnp.float32
    )
    grad_act = jnp.einsum(
        "cnd,fd->cnf", grad_branch, weight_down, preferred_element_type=jnp.float32
    )
    unused, gelu_pull = jax.vjp(partial(jax.nn.gelu, approximate=True), pre_act)
    grad_pre = gelu_pull(grad_act)[0].astype(jnp.bfloat16)
    grad_weight_up = jnp.einsum("cnd,cnf->df", hidden, grad_pre, preferred_element_type=jnp.float32)
    grad_bias_up = jnp.sum(grad_pre.astype(jnp.float32), axis=(0, 1))
    grad_hidden = join_back(
        jnp.einsum("cnf,df->cnd", grad_pre, weight_up, preferred_element_type=jnp.float32)
    )
    unused_too, norm_pull = jax.vjp(normed, tensor, gain_row, shift_row)
    grad_tensor, grad_gain, grad_shift = norm_pull(grad_hidden)
    return (grad_tensor, grad_weight_up, grad_bias_up, grad_weight_down, grad_gain, grad_shift)


def local(
    tokens,
    frames,
    text_mask,
    latents,
    cross_q,
    cross_kv,
    cross_out,
    cross_up,
    cross_down,
    self_qkv,
    self_out,
    self_up,
    self_down,
    head_bias,
    up_bias,
    out_bias,
    norm_gain,
    norm_bias,
    latents_cot,
):
    head_index = lax.axis_index("head")
    head_width = cross_q.shape[0]
    heads_here = head_width // HD
    scaling = HD ** (-0.5)
    clips_here = tokens.shape[0]
    rows_here = tokens.shape[1]
    length = rows_here * lax.axis_size("head")
    position = jnp.arange(length, dtype=jnp.int32)
    text_full = jnp.concatenate(
        [jnp.zeros((clips_here, F_MAX * P_SIZE), jnp.int32), text_mask], axis=1
    )
    usable = (position[None, :] < frames[:, None] * P_SIZE) | (text_full == 1)
    gathered, weights_whole = (
        lax.all_gather(tokens, "head", axis=1, tiled=True),
        lax.all_gather(cross_kv, "head", axis=1, tiled=True),
    )
    full_rows = gathered.astype(jnp.float32)
    row_mean = jnp.mean(full_rows, axis=-1, keepdims=True)
    centered = full_rows - row_mean
    inverse = lax.rsqrt(jnp.mean(centered * centered, axis=-1, keepdims=True) + EPSILON)
    inputs = (centered * inverse * norm_gain[0] + norm_bias[0]).astype(jnp.bfloat16)
    key_value = jnp.einsum("cld,kwd->clkw", inputs, cross_kv, preferred_element_type=jnp.float32)
    key_rows = key_value[:, :, 0].astype(jnp.bfloat16)
    cross_values = (key_value[:, :, 1] + head_bias[0, 1]).astype(jnp.bfloat16)
    start_state = latents.astype(jnp.float32)
    latent_norm = normed(start_state, norm_gain[1], norm_bias[1]).astype(jnp.bfloat16)
    cross_queries = (
        (
            jnp.einsum("cnd,wd->cnw", latent_norm, cross_q, preferred_element_type=jnp.float32)
            + head_bias[0, 0]
        )
        * scaling
    ).astype(jnp.bfloat16)
    cross_parts = (
        split_heads(cross_queries, heads_here),
        split_heads(key_rows, heads_here),
        split_heads(cross_values, heads_here),
        usable,
    )
    cross_mix, cross_max, cross_totals = lax.map(attend_parts, cross_parts)
    cross_flat = merge_heads(cross_mix)
    after_cross = (
        start_state
        + join_heads(
            jnp.einsum("cnw,wd->cnd", cross_flat, cross_out, preferred_element_type=jnp.float32)
        )
        + out_bias[0, 0]
    )
    cross_branch, cross_saved = feed_forward(
        after_cross, norm_gain[2], norm_bias[2], cross_up, up_bias[0], cross_down
    )
    after_mlp = after_cross + cross_branch + out_bias[0, 1]
    self_norm = normed(after_mlp, norm_gain[3], norm_bias[3]).astype(jnp.bfloat16)
    triple = jnp.einsum("cnd,kwd->cnkw", self_norm, self_qkv, preferred_element_type=jnp.float32)
    self_queries = ((triple[:, :, 0] + head_bias[1, 0]) * scaling).astype(jnp.bfloat16)
    self_keys = triple[:, :, 1].astype(jnp.bfloat16)
    self_values = (triple[:, :, 2] + head_bias[1, 1]).astype(jnp.bfloat16)
    everyone = jnp.ones((clips_here, self_keys.shape[1]), dtype=bool)
    self_parts = (
        split_heads(self_queries, heads_here),
        split_heads(self_keys, heads_here),
        split_heads(self_values, heads_here),
        everyone,
    )
    self_mix, self_max, self_totals = lax.map(attend_parts, self_parts)
    self_flat = merge_heads(self_mix)
    after_self = (
        after_mlp
        + join_heads(
            jnp.einsum("cnw,wd->cnd", self_flat, self_out, preferred_element_type=jnp.float32)
        )
        + out_bias[1, 0]
    )
    self_branch, self_saved = feed_forward(
        after_self, norm_gain[4], norm_bias[4], self_up, up_bias[1], self_down
    )
    latents_out = after_self + self_branch + out_bias[1, 1]
    bias_self_mlp = jnp.sum(latents_cot, axis=(0, 1))
    grad_ln_four, grad_self_up, upbias_self, grad_self_down, gain_four, shift_four = feed_back(
        after_self, norm_gain[4], norm_bias[4], self_up, self_down, self_saved, latents_cot
    )
    grad_state = latents_cot + grad_ln_four
    bias_self_attn = jnp.sum(grad_state, axis=(0, 1))
    grad_attn_in = grad_state.astype(jnp.bfloat16)
    grad_self_out = jnp.einsum(
        "cnw,cnd->wd", self_flat, grad_attn_in, preferred_element_type=jnp.float32
    )
    grad_mix = jnp.einsum(
        "cnd,wd->cnw", grad_attn_in, self_out, preferred_element_type=jnp.float32
    ).astype(jnp.bfloat16)
    self_grads = lax.map(
        back_parts, self_parts + (self_max, self_totals, split_heads(grad_mix, heads_here))
    )
    grad_query_scaled = (merge_heads(self_grads[0]).astype(jnp.float32) * scaling).astype(
        jnp.bfloat16
    )
    grad_triple = jnp.stack(
        [grad_query_scaled, merge_heads(self_grads[1]), merge_heads(self_grads[2])], axis=2
    )
    grad_self_qkv = jnp.einsum(
        "cnd,cnkw->kwd", self_norm, grad_triple, preferred_element_type=jnp.float32
    )
    bias_self_q = jnp.sum(grad_triple[:, :, 0].astype(jnp.float32), axis=(0, 1))
    bias_self_v = jnp.sum(grad_triple[:, :, 2].astype(jnp.float32), axis=(0, 1))
    grad_self_in = join_back(
        jnp.einsum("cnkw,kwd->cnd", grad_triple, self_qkv, preferred_element_type=jnp.float32)
    )
    unused, norm_pull = jax.vjp(normed, after_mlp, norm_gain[3], norm_bias[3])
    grad_ln_three, gain_three, shift_three = norm_pull(grad_self_in)
    grad_state = grad_state + grad_ln_three
    bias_cross_mlp = jnp.sum(grad_state, axis=(0, 1))
    grad_ln_two, grad_cross_up, upbias_cross, grad_cross_down, gain_two, shift_two = feed_back(
        after_cross, norm_gain[2], norm_bias[2], cross_up, cross_down, cross_saved, grad_state
    )
    grad_state = grad_state + grad_ln_two
    bias_cross_attn = jnp.sum(grad_state, axis=(0, 1))
    grad_attn_in = grad_state.astype(jnp.bfloat16)
    grad_cross_out = jnp.einsum(
        "cnw,cnd->wd", cross_flat, grad_attn_in, preferred_element_type=jnp.float32
    )
    grad_mix = jnp.einsum(
        "cnd,wd->cnw", grad_attn_in, cross_out, preferred_element_type=jnp.float32
    ).astype(jnp.bfloat16)
    cross_grads = lax.map(
        back_parts, cross_parts + (cross_max, cross_totals, split_heads(grad_mix, heads_here))
    )
    grad_query_cross = (merge_heads(cross_grads[0]).astype(jnp.float32) * scaling).astype(
        jnp.bfloat16
    )
    grad_cross_q = jnp.einsum(
        "cnd,cnw->wd", latent_norm, grad_query_cross, preferred_element_type=jnp.float32
    )
    bias_cross_q = jnp.sum(grad_query_cross.astype(jnp.float32), axis=(0, 1))
    grad_latent_in = join_back(
        jnp.einsum("cnw,wd->cnd", grad_query_cross, cross_q, preferred_element_type=jnp.float32)
    )
    unused_too, latent_pull = jax.vjp(normed, start_state, norm_gain[1], norm_bias[1])
    grad_ln_one, gain_one, shift_one = latent_pull(grad_latent_in)
    grad_latents = grad_state + grad_ln_one
    grad_pair = jnp.stack([merge_heads(cross_grads[1]), merge_heads(cross_grads[2])], axis=2)
    grad_cross_kv = jnp.einsum(
        "cld,clkw->kwd", inputs, grad_pair, preferred_element_type=jnp.float32
    )
    bias_cross_v = jnp.sum(grad_pair[:, :, 1].astype(jnp.float32), axis=(0, 1))
    arrived = lax.all_to_all(grad_pair, "head", split_axis=1, concat_axis=3, tiled=True)
    grad_share = jnp.einsum(
        "clkw,kwd->cld", arrived, weights_whole, preferred_element_type=jnp.float32
    )
    own_start = head_index * rows_here
    own_mean = lax.dynamic_slice_in_dim(row_mean, own_start, rows_here, 1)
    own_inverse = lax.dynamic_slice_in_dim(inverse, own_start, rows_here, 1)
    standard = (tokens.astype(jnp.float32) - own_mean) * own_inverse
    scaled = grad_share * norm_gain[0]
    mean_plain = jnp.mean(scaled, axis=-1, keepdims=True)
    mean_cross = jnp.mean(scaled * standard, axis=-1, keepdims=True)
    grad_tokens = (own_inverse * (scaled - mean_plain - standard * mean_cross)).astype(jnp.bfloat16)
    gain_zero, shift_zero = lax.psum(
        (jnp.sum(grad_share * standard, axis=(0, 1)), jnp.sum(grad_share, axis=(0, 1))), "head"
    )
    grad_head_bias = jnp.stack(
        [jnp.stack([bias_cross_q, bias_cross_v]), jnp.stack([bias_self_q, bias_self_v])]
    )
    grad_up_bias = jnp.stack([upbias_cross, upbias_self])
    out_full = jnp.stack(
        [jnp.stack([bias_cross_attn, bias_cross_mlp]), jnp.stack([bias_self_attn, bias_self_mlp])]
    )
    grad_out_bias = share_of(out_full, head_index, head_width)
    grad_norm_gain = share_of(
        jnp.stack([gain_zero, gain_one, gain_two, gain_three, gain_four]), head_index, head_width
    )
    grad_norm_bias = share_of(
        jnp.stack([shift_zero, shift_one, shift_two, shift_three, shift_four]),
        head_index,
        head_width,
    )
    small_sums = lax.psum(
        (grad_head_bias, grad_up_bias, grad_out_bias, grad_norm_gain, grad_norm_bias), "dp"
    )
    combined = (
        lax.psum_scatter(grad_cross_q, "dp", scatter_dimension=1, tiled=True),
        lax.psum_scatter(grad_cross_kv, "dp", scatter_dimension=2, tiled=True),
        lax.psum_scatter(grad_cross_out, "dp", scatter_dimension=1, tiled=True),
        lax.psum_scatter(grad_cross_up, "dp", scatter_dimension=0, tiled=True),
        lax.psum_scatter(grad_cross_down, "dp", scatter_dimension=1, tiled=True),
        lax.psum_scatter(grad_self_qkv, "dp", scatter_dimension=2, tiled=True),
        lax.psum_scatter(grad_self_out, "dp", scatter_dimension=1, tiled=True),
        lax.psum_scatter(grad_self_up, "dp", scatter_dimension=0, tiled=True),
        lax.psum_scatter(grad_self_down, "dp", scatter_dimension=1, tiled=True),
    )
    cross_sums = combined[:5]
    self_sums = combined[5:]
    return (
        latents_out,
        grad_tokens,
        grad_latents,
        cross_sums[0],
        cross_sums[1],
        cross_sums[2],
        cross_sums[3],
        cross_sums[4],
        self_sums[0],
        self_sums[1],
        self_sums[2],
        self_sums[3],
        small_sums[0],
        small_sums[1],
        small_sums[2],
        small_sums[3],
        small_sums[4],
    )


def solution(mesh):
    in_specs = (
        P("dp", "head", None),
        P("dp"),
        P("dp", None),
        P("dp", None, None),
        P("head", None),
        P(None, "head", None),
        P("head", None),
        P(None, "head"),
        P("head", None),
        P(None, "head", None),
        P("head", None),
        P(None, "head"),
        P("head", None),
        P(None, None, "head"),
        P(None, "head"),
        P(),
        P(),
        P(),
        P("dp", None, None),
    )
    out_specs = (
        P("dp", None, None),
        P("dp", "head", None),
        P("dp", None, None),
        P("head", "dp"),
        P(None, "head", "dp"),
        P("head", "dp"),
        P("dp", "head"),
        P("head", "dp"),
        P(None, "head", "dp"),
        P("head", "dp"),
        P("dp", "head"),
        P("head", "dp"),
        P(None, None, "head"),
        P(None, "head"),
        P(None, None, "head"),
        P(None, "head"),
        P(None, "head"),
    )
    return jax.shard_map(local, mesh=mesh, in_specs=in_specs, out_specs=out_specs, check_vma=False)
```

profile of v0, /device:TPU:0, one launch (start us, length us, event | category | flops | bytes accessed | tf_op | source)
XLA Modules:
  0.0 1166.3 jit_solution(2360226538765348507)
XLA Ops:
  7.3 18.4 %copy.55 = bf16[1,1578,768]{2,0,1:T(2,128)(2,1)} copy(bf16[1,1578,768]{2,1,0:T(8,128)(2,1)} %param.19) | data formatting | bytes 4847616 | tf_op args[0]
  28.8 122.7 %all-gather.3.cloned.1.call-done = bf16[1,6312,768]{2,0,1:T(2,128)(2,1)} async-done(((bf16[1,1578,768]{2,0,1:T(2,128)(2,1)}), bf16[1,6312,768]{2,0,1:T(2,128)(2,1)}) %all-gather.3.cloned.1.call-update) | async-done | bytes 9695248 | tf_op jit(solution)/shard_map/all_gather | solution.py:146
  159.0 14.1 %fusion.4 = f32[6312]{0:T(1024)S(1)} fusion(f32[6312]{0:T(1024)S(1)} %broadcast_multiply_fusion, bf16[1,6312,768]{2,0,1:T(2,128)(2,1)} %all-gather.3.cloned.1.call-done), kind=kLoop, calls=%fused_computation.6 | loop fusion | flops 19384152 | bytes 9745728 | tf_op jit(solution)/shard_map/reduce_sum | solution.py:152
  201.4 31.3 %all-reduce.12.cloned.1.call-done = bf16[1,128,768]{2,1,0:T(8,128)(2,1)} async-done(((bf16[1,128,768]{2,1,0:T(8,128)(2,1)}), bf16[1,128,768]{2,1,0:T(8,128)(2,1)}) %all-reduce.12.cloned.1.call-update) | async-done | bytes 196624 | tf_op jit(solution)/shard_map/psum | solution.py:36
  239.6 30.8 %all-reduce.14.cloned.1.call-done = bf16[1,128,768]{2,1,0:T(8,128)(2,1)} async-done(((bf16[1,128,768]{2,1,0:T(8,128)(2,1)}), bf16[1,128,768]{2,1,0:T(8,128)(2,1)}) %all-reduce.14.cloned.1.call-update) | async-done | bytes 196624 | tf_op jit(solution)/shard_map/psum | solution.py:36
  280.2 32.1 %all-reduce.16.cloned.1.call-done = bf16[1,128,768]{2,1,0:T(8,128)(2,1)} async-done(((bf16[1,128,768]{2,1,0:T(8,128)(2,1)}), bf16[1,128,768]{2,1,0:T(8,128)(2,1)}) %all-reduce.16.cloned.1.call-update) | async-done | bytes 196624 | tf_op jit(solution)/shard_map/psum | solution.py:36
  320.6 32.1 %all-reduce.18.cloned.1.call-done = bf16[1,128,768]{2,1,0:T(8,128)(2,1)} async-done(((bf16[1,128,768]{2,1,0:T(8,128)(2,1)}), bf16[1,128,768]{2,1,0:T(8,128)(2,1)}) %all-reduce.18.cloned.1.call-update) | async-done | bytes 196624 | tf_op jit(solution)/shard_map/psum | solution.py:40
  369.2 32.1 %all-reduce.20.cloned.1.call-done = bf16[1,128,768]{2,1,0:T(8,128)(2,1)} async-done(((bf16[1,128,768]{2,1,0:T(8,128)(2,1)}), bf16[1,128,768]{2,1,0:T(8,128)(2,1)}) %all-reduce.20.cloned.1.call-update) | async-done | bytes 196624 | tf_op jit(solution)/shard_map/psum | solution.py:40
  412.8 29.3 %all-reduce.22.cloned.1.call-done = bf16[1,128,768]{2,1,0:T(8,128)(2,1)} async-done(((bf16[1,128,768]{2,1,0:T(8,128)(2,1)}), bf16[1,128,768]{2,1,0:T(8,128)(2,1)}) %all-reduce.22.cloned.1.call-update) | async-done | bytes 196624 | tf_op jit(solution)/shard_map/psum | solution.py:40
  447.5 11.8 %multiply_reduce_fusion = (f32[3,128]{1,0:T(4,128)S(1)}, f32[3,128,6312]{1,2,0:T(8,128)}) fusion(f32[3,128,6312]{1,2,0:T(8,128)} %get-tuple-element.188, f32[3,128]{1,0:T(4,128)S(1)} %copy-done.84, bf16[128,3,64]{0,2,1:T(8,128)(2,1)S(1)} %bitcast.256, f32[6312,3,64]{0,2,1:T(8,128)} %bitcast.227, f32[3,64]{1,0:T(4,128)S(1)} %copy-done.93), kind=kOutput, calls=%fused_computation.16 | convolution fusion | flops 319942272 | bytes 24291072 | tf_op jit(solution)/shard_map/while/body/eval_jaxpr/qhe,khe->hqk/dot_general | solution.py:67
  459.3 9.9 multiply_convert_fusion
  529.6 16.4 %copy.61 = bf16[1,6312,2,192]{3,2,0,1:T(2,128)(2,1)} copy(bf16[1,6312,2,192]{1,3,2,0:T(8,128)(2,1)} %pad_maximum_fusion) | data formatting | bytes 9695232 | tf_op jit(solution)/shard_map/stack | solution.py:272
  560.5 13.6 %reduce-scatter.36.cloned.1.call-done = f32[96,192]{1,0:T(8,128)} async-done(((f32[768,192]{1,0:T(8,128)}), f32[96,192]{1,0:T(8,128)}) %reduce-scatter.36.cloned.1.call-update) | async-done | bytes 73744
  575.7 63.7 %reduce-scatter.28.cloned.1.call-done = f32[96,192]{1,0:T(8,128)} async-done(((f32[768,192]{1,0:T(8,128)}), f32[96,192]{1,0:T(8,128)}) %reduce-scatter.28.cloned.1.call-update) | async-done | bytes 73744
  641.1 64.0 %reduce-scatter.32.cloned.1.call-done = f32[96,192]{1,0:T(8,128)} async-done(((f32[768,192]{1,0:T(8,128)}), f32[96,192]{1,0:T(8,128)}) %reduce-scatter.32.cloned.1.call-update) | async-done | bytes 73744
  706.7 65.4 %reduce-scatter.30.cloned.1.call-done = f32[96,384]{1,0:T(8,128)} async-done(((f32[768,384]{1,0:T(8,128)}), f32[96,384]{1,0:T(8,128)}) %reduce-scatter.30.cloned.1.call-update) | async-done | bytes 147472
  774.0 68.6 %reduce-scatter.34.cloned.1.call-done = f32[96,576]{1,0:T(8,128)} async-done(((f32[768,576]{1,0:T(8,128)}), f32[96,576]{1,0:T(8,128)}) %reduce-scatter.34.cloned.1.call-update) | async-done | bytes 221200
  844.6 17.2 %copy.62 = bf16[1,4,1578,2,192]{2,4,1,3,0:T(8,128)(2,1)} copy(bf16[1,4,1578,2,192]{4,3,2,1,0:T(2,128)(2,1)} %bitcast.46) | data formatting | bytes 9695232 | tf_op jit(solution)/shard_map/all_to_all | solution.py:277
  867.0 9.0 fusion.13
  885.4 37.7 %all-reduce.1 = (f32[2,2,192]{2,1,0:T(2,128)}, f32[2,768]{1,0:T(2,128)}, f32[2,2,192]{2,1,0:T(2,128)}, f32[5,192]{1,0:T(8,128)}, f32[5,192]{1,0:T(8,128)}) all-reduce(f32[2,2,192]{2,1,0:T(2,128)S(1)} %pad_maximum_fusion.2, f32[2,768]{1,0:T(2,128)S(1)} %pad_maximum_fusion.1, ...), channel_id=1, replica_groups=mesh['dp'=8,'head'=4] {'dp'}, use_global_device_ids=true, to_apply=%region_47.48 | all-reduce | flops 4992 | bytes 39936 | tf_op jit(solution)/shard_map/psum | solution.py:308
  928.4 12.5 %reduce-scatter.24.cloned.1.call-done = f32[96,768]{1,0:T(8,128)} async-done(((f32[768,768]{1,0:T(8,128)}), f32[96,768]{1,0:T(8,128)}) %reduce-scatter.24.cloned.1.call-update) | async-done | bytes 294928 | tf_op jit(solution)/shard_map/reduce_scatter | solution.py:319
  940.9 72.7 %reduce-scatter.26.cloned.1.call-done = f32[768,96]{0,1:T(8,128)} async-done(((f32[768,768]{0,1:T(8,128)}), f32[768,96]{0,1:T(8,128)}) %reduce-scatter.26.cloned.1.call-update) | async-done | bytes 294928 | tf_op jit(solution)/shard_map/reduce_scatter | solution.py:320
  1013.6 72.9 %reduce-scatter.20.cloned.1.call-done = f32[96,768]{1,0:T(8,128)} async-done(((f32[768,768]{1,0:T(8,128)}), f32[96,768]{1,0:T(8,128)}) %reduce-scatter.20.cloned.1.call-update) | async-done | bytes 294928 | tf_op jit(solution)/shard_map/reduce_scatter | solution.py:315
  1086.5 72.8 %reduce-scatter.22.cloned.1.call-done = f32[768,96]{0,1:T(8,128)} async-done(((f32[768,768]{0,1:T(8,128)}), f32[768,96]{0,1:T(8,128)}) %reduce-scatter.22.cloned.1.call-update) | async-done | bytes 294928 | tf_op jit(solution)/shard_map/reduce_scatter | solution.py:316
  (381 shorter events, 198.4 us)
Async XLA Ops:
  7.2 229.9 %copy-start = (bf16[768,768]{1,0:T(8,128)(2,1)S(1)}, bf16[768,768]{1,0:T(8,128)(2,1)}, u32[]{:S(2)}) copy-start(bf16[768,768]{1,0:T(8,128)(2,1)} %param.27) | copy-start | bytes 3538948
  7.3 144.2 %all-gather.3.cloned.1.call-start = ((), (), s32[]{:S(2)}) async-start(), calls=%async_computation.10 | async-start | bytes 24238080 | tf_op jit(solution)/shard_map/all_gather | solution.py:146
  25.7 207.0 %all-reduce.12.cloned.1.call-start = ((), (), s32[]{:S(2)}) async-start(), calls=%async_computation.11 | async-start | bytes 393216 | tf_op jit(solution)/shard_map/psum | solution.py:36
  25.9 168.6 %copy-start.92 = (f32[3,64]{1,0:T(4,128)}, f32[3,64]{1,0:T(4,128)S(1)}, u32[]{:S(2)}) copy-start(f32[3,64]{1,0:T(4,128)S(1)} %add.344) | copy-start | bytes 2308
  27.9 207.1 %copy-start.47 = (f32[768]{0:T(1024)}, f32[768]{0:T(1024)S(1)}, u32[]{:S(2)}) copy-start(f32[768]{0:T(1024)S(1)} %get-tuple-element.151) | copy-start | bytes 9220
  28.7 154.8 %copy-start.35 = (bf16[128,192]{0,1:T(8,128)(2,1)}, bf16[128,192]{0,1:T(8,128)(2,1)S(1)}, u32[]{:S(2)}) copy-start(bf16[128,192]{0,1:T(8,128)(2,1)S(1)} %fusion.33) | copy-start | bytes 147460
  200.6 69.8 %all-reduce.14.cloned.1.call-start = ((), (), s32[]{:S(2)}) async-start(), calls=%async_computation.12 | async-start | bytes 393216 | tf_op jit(solution)/shard_map/psum | solution.py:36
  238.2 74.1 %all-reduce.16.cloned.1.call-start = ((), (), s32[]{:S(2)}) async-start(), calls=%async_computation.13 | async-start | bytes 393216 | tf_op jit(solution)/shard_map/psum | solution.py:36
  280.1 72.6 %all-reduce.18.cloned.1.call-start = ((), (), s32[]{:S(2)}) async-start(), calls=%async_computation.14 | async-start | bytes 393216 | tf_op jit(solution)/shard_map/psum | solution.py:40
  320.6 80.8 %all-reduce.20.cloned.1.call-start = ((), (), s32[]{:S(2)}) async-start(), calls=%async_computation.15 | async-start | bytes 393216 | tf_op jit(solution)/shard_map/psum | solution.py:40
  369.1 72.9 %all-reduce.22.cloned.1.call-start = ((), (), s32[]{:S(2)}) async-start(), calls=%async_computation.16 | async-start | bytes 393216 | tf_op jit(solution)/shard_map/psum | solution.py:40
  409.9 146.2 %all-reduce.24.cloned.1.call-start = ((), (), s32[]{:S(2)}) async-start(), calls=%async_computation.27 | async-start | bytes 786432 | tf_op jit(solution)/shard_map/psum | solution.py:36
  474.5 99.6 %reduce-scatter.36.cloned.1.call-start = ((), (), s32[]{:S(2)}) async-start(), calls=%async_computation.26 | async-start | bytes 884736
  475.8 163.7 %reduce-scatter.28.cloned.1.call-start = ((), (), s32[]{:S(2)}) async-start(), calls=%async_computation.22 | async-start | bytes 884736
  478.4 226.7 %reduce-scatter.32.cloned.1.call-start = ((), (), s32[]{:S(2)}) async-start(), calls=%async_computation.24 | async-start | bytes 884736
  485.4 286.7 %reduce-scatter.30.cloned.1.call-start = ((), (), s32[]{:S(2)}) async-start(), calls=%async_computation.23 | async-start | bytes 1327104
  506.9 335.6 %reduce-scatter.34.cloned.1.call-start = ((), (), s32[]{:S(2)}) async-start(), calls=%async_computation.25 | async-start | bytes 2211840
  517.7 349.4 %all-gather.5.cloned.1.call-start = ((), (), s32[]{:S(2)}) async-start(), calls=%async_computation.17 | async-start | bytes 2949120 | tf_op jit(solution)/shard_map/all_gather | solution.py:147
  518.3 422.6 %reduce-scatter.24.cloned.1.call-start = ((), (), s32[]{:S(2)}) async-start(), calls=%async_computation.20 | async-start | bytes 2654208 | tf_op jit(solution)/shard_map/reduce_scatter | solution.py:319
  520.4 493.2 %reduce-scatter.26.cloned.1.call-start = ((), (), s32[]{:S(2)}) async-start(), calls=%async_computation.21 | async-start | bytes 2654208 | tf_op jit(solution)/shard_map/reduce_scatter | solution.py:320
  522.4 564.1 %reduce-scatter.20.cloned.1.call-start = ((), (), s32[]{:S(2)}) async-start(), calls=%async_computation.18 | async-start | bytes 2654208 | tf_op jit(solution)/shard_map/reduce_scatter | solution.py:315
  546.1 298.5 %all-to-all-start = ((bf16[1,6312,2,192]{3,2,0,1:T(2,128)(2,1)}), bf16[1,6312,2,192]{3,2,0,1:T(2,128)(2,1)}, u32[]{:S(2)}, u32[]{:S(2)}) async-start(bf16[1,6312,2,192]{3,2,0,1:T(2,128)(2,1)} %copy.61), calls=%async_computation | async-start | bytes 12926976 | tf_op jit(solution)/shard_map/all_to_all | solution.py:277
  551.5 607.7 %reduce-scatter.22.cloned.1.call-start = ((), (), s32[]{:S(2)}) async-start(), calls=%async_computation.19 | async-start | bytes 2654208 | tf_op jit(solution)/shard_map/reduce_scatter | solution.py:316
  923.1 236.1 %copy-start.1 = (bf16[768,768]{1,0:T(8,128)(2,1)S(1)}, bf16[768,768]{1,0:T(8,128)(2,1)}, u32[]{:S(2)}) copy-start(bf16[768,768]{1,0:T(8,128)(2,1)} %param.27) | copy-start | bytes 3538948
  (96 other events, 2352.8 us)
Sparse Core Ops, SparseCore 0:
  25.9 125.5 all-gather.2
  200.7 31.9 all-reduce.11
  238.3 32.0 all-reduce.13
  280.2 32.0 all-reduce.15
  320.7 32.0 all-reduce.17
  369.2 32.0 all-reduce.19
  410.0 32.0 all-reduce.21
  474.6 32.8 all-reduce.23
  510.8 63.2 reduce-scatter.35
  577.3 62.1 reduce-scatter.27
  642.8 62.2 reduce-scatter.31
  708.3 63.7 reduce-scatter.29
  776.1 66.3 reduce-scatter.33
  844.0 22.9 all-gather.4
  870.9 69.9 reduce-scatter.23
  944.8 68.7 reduce-scatter.25
  1017.5 68.9 reduce-scatter.19
  1090.4 68.7 reduce-scatter.21
where the time goes:
time: 1170 us
  waiting for transfers between devices  823 us (70%)
  matrix products  102 us (9%)
  local copies, waits for them, and re-layouts  92.2 us (8%)
  other arithmetic  81.6 us (7%)
  blocking collectives  44.1 us (4%)
  between operations  16.7 us (1%)
    unnamed x23, waiting for transfers between devices  276 us
    all_gather x1, waiting for transfers between devices, local(): lax.all_gather(tokens, 'head', axis=1, tiled=True)  123 us
    psum x4, waiting for transfers between devices, join_heads(): lax.psum(partial_sum.astype(jnp.bfloat16), 'head').astype(jnp.float32)  94.2 us
    psum x3, waiting for transfers between devices, join_back(): lax.psum(partial_sum.astype(jnp.bfloat16), 'head').astype(jnp.float32)  93.6 us
    reduce_scatter x1, waiting for transfers between devices, local(): lax.psum_scatter(grad_cross_up, 'dp', scatter_dimension=0, tiled=True)  72.9 us
    reduce_scatter x1, waiting for transfers between devices, local(): lax.psum_scatter(grad_cross_down, 'dp', scatter_dimension=1, tiled=True)  72.8 us
    reduce_scatter x1, waiting for transfers between devices, local(): lax.psum_scatter(grad_self_down, 'dp', scatter_dimension=1, tiled=True)  72.7 us
    unnamed x214, local copies, waits for them, and re-layouts  51.9 us
  transfers between devices with their start and end apart: 19, of which 17 were waited for; matrix products, arithmetic and copies ran while one was open for 11% of the time, Pallas kernels for 0%

commit v1 on v0

--- a/solution.py
+++ b/solution.py
@@ -37,7 +37,9 @@
 
 
 def join_back(partial_sum):
-    return lax.psum(partial_sum.astype(jnp.bfloat16), "head").astype(jnp.float32)
+    return jnp.sum(lax.all_gather(partial_sum.astype(jnp.bfloat16), "head"), axis=0).astype(
+        jnp.float32
+    )
 
 
 def scores_of(queries, key_rows, usable):

time: 1170 us -> 1080 us (0.923)
  waiting for transfers between devices: 823 us -> 644 us
  blocking collectives: 44.1 us -> 142 us
    unnamed x23 -> x20, waiting for transfers between devices: 276 us -> 157 us
    all_gather x0 -> x4, blocking collectives: none -> 97.9 us  [join_back(): lax.all_gather(partial_sum.astype(jnp.bfloat16), 'head')]
    psum x3 -> x0, waiting for transfers between devices: 93.6 us -> none  [join_back(): lax.psum(partial_sum.astype(jnp.bfloat16), 'head').astype(jnp.float32)]
    psum x4, waiting for transfers between devices: 94.2 us -> 128 us  [join_heads(): lax.psum(partial_sum.astype(jnp.bfloat16), 'head').astype(jnp.float32)]
    unnamed x214 -> x216, local copies, waits for them, and re-layouts: 51.9 us -> 50 us
  transfers between devices with their start and end apart: 19 -> 16, of which waited for: 17 -> 13; matrix products, arithmetic and copies ran while one was open for 11% -> 12% of each run, Pallas kernels for 0% -> 0%
where the time goes in v1:
time: 1080 us; the launch traced here: 1070 us
  waiting for transfers between devices  644 us (60%)
  blocking collectives  142 us (13%)
  matrix products  99.3 us (9%)
  local copies, waits for them, and re-layouts  90.3 us (8%)
  other arithmetic  76.4 us (7%)
  between operations  16.4 us (2%)
    unnamed x20, waiting for transfers between devices  157 us
    psum x4, waiting for transfers between devices, join_heads(): lax.psum(partial_sum.astype(jnp.bfloat16), 'head').astype(jnp.float32)  128 us
    all_gather x1, waiting for transfers between devices, local(): lax.all_gather(tokens, 'head', axis=1, tiled=True)  123 us
    all_gather x4, blocking collectives, join_back(): lax.all_gather(partial_sum.astype(jnp.bfloat16), 'head')  97.9 us
    reduce_scatter x1, waiting for transfers between devices, local(): lax.psum_scatter(grad_self_down, 'dp', scatter_dimension=1, tiled=True)  72.9 us
    reduce_scatter x1, waiting for transfers between devices, local(): lax.psum_scatter(grad_cross_down, 'dp', scatter_dimension=1, tiled=True)  72.8 us
    reduce_scatter x1, waiting for transfers between devices, local(): lax.psum_scatter(grad_cross_up, 'dp', scatter_dimension=0, tiled=True)  72.7 us
    unnamed x216, local copies, waits for them, and re-layouts  50 us
  transfers between devices with their start and end apart: 16, of which 13 were waited for; matrix products, arithmetic and copies ran while one was open for 12% of the time, Pallas kernels for 0%

profile of v1, /device:TPU:0, one launch (start us, length us, event | category | flops | bytes accessed | tf_op | source)
XLA Modules:
  0.0 1074.7 jit_solution(3774645359340739131)
XLA Ops:
  7.3 18.4 %copy.55 = bf16[1,1578,768]{2,0,1:T(2,128)(2,1)} copy(bf16[1,1578,768]{2,1,0:T(8,128)(2,1)} %param.19) | data formatting | bytes 4847616 | tf_op args[0]
  28.7 122.7 %all-gather.7.cloned.1.call-done = bf16[1,6312,768]{2,0,1:T(2,128)(2,1)} async-done(((bf16[1,1578,768]{2,0,1:T(2,128)(2,1)}), bf16[1,6312,768]{2,0,1:T(2,128)(2,1)}) %all-gather.7.cloned.1.call-update) | async-done | bytes 9695248 | tf_op jit(solution)/shard_map/all_gather | solution.py:148
  159.0 14.1 %fusion.4 = f32[6312]{0:T(1024)S(1)} fusion(f32[6312]{0:T(1024)S(1)} %broadcast_multiply_fusion, bf16[1,6312,768]{2,0,1:T(2,128)(2,1)} %all-gather.7.cloned.1.call-done), kind=kLoop, calls=%fused_computation.6 | loop fusion | flops 19384152 | bytes 9745728 | tf_op jit(solution)/shard_map/reduce_sum | solution.py:154
  200.9 31.3 %all-reduce.8.cloned.1.call-done = bf16[1,128,768]{2,1,0:T(8,128)(2,1)} async-done(((bf16[1,128,768]{2,1,0:T(8,128)(2,1)}), bf16[1,128,768]{2,1,0:T(8,128)(2,1)}) %all-reduce.8.cloned.1.call-update) | async-done | bytes 196624 | tf_op jit(solution)/shard_map/psum | solution.py:36
  240.4 30.8 %all-reduce.10.cloned.1.call-done = bf16[1,128,768]{2,1,0:T(8,128)(2,1)} async-done(((bf16[1,128,768]{2,1,0:T(8,128)(2,1)}), bf16[1,128,768]{2,1,0:T(8,128)(2,1)}) %all-reduce.10.cloned.1.call-update) | async-done | bytes 196624 | tf_op jit(solution)/shard_map/psum | solution.py:36
  280.9 32.1 %all-reduce.12.cloned.1.call-done = bf16[1,128,768]{2,1,0:T(8,128)(2,1)} async-done(((bf16[1,128,768]{2,1,0:T(8,128)(2,1)}), bf16[1,128,768]{2,1,0:T(8,128)(2,1)}) %all-reduce.12.cloned.1.call-update) | async-done | bytes 196624 | tf_op jit(solution)/shard_map/psum | solution.py:36
  331.3 33.5 %all-reduce.14.cloned.1.call-done = bf16[1,128,768]{2,1,0:T(8,128)(2,1)} async-done(((bf16[1,128,768]{2,1,0:T(8,128)(2,1)}), bf16[1,128,768]{2,1,0:T(8,128)(2,1)}) %all-reduce.14.cloned.1.call-update) | async-done | bytes 196624 | tf_op jit(solution)/shard_map/psum | solution.py:36
  375.0 7.7 all-gather.1
  389.7 9.4 all-gather.2
  406.1 11.8 %multiply_reduce_fusion = (f32[3,128]{1,0:T(4,128)S(1)}, f32[3,128,6312]{1,2,0:T(8,128)}) fusion(f32[3,128,6312]{1,2,0:T(8,128)} %get-tuple-element.179, f32[3,128]{1,0:T(4,128)} %copy-done.84, bf16[128,3,64]{0,2,1:T(8,128)(2,1)S(1)} %bitcast.337, f32[6312,3,64]{0,2,1:T(8,128)} %bitcast.304, f32[3,64]{1,0:T(4,128)} %copy-done.93), kind=kOutput, calls=%fused_computation.16 | convolution fusion | flops 319942272 | bytes 24291072 | tf_op jit(solution)/shard_map/while/body/eval_jaxpr/qhe,khe->hqk/dot_general | solution.py:69
  418.0 9.9 multiply_convert_fusion
  447.6 8.9 fusion.11
  486.3 16.4 %copy.61 = bf16[1,6312,2,192]{3,2,0,1:T(2,128)(2,1)} copy(bf16[1,6312,2,192]{1,3,2,0:T(8,128)(2,1)} %pad_maximum_fusion) | data formatting | bytes 9695232 | tf_op jit(solution)/shard_map/stack | solution.py:274
  512.2 73.4 %all-gather.3 = bf16[512,768]{1,0:T(8,128)(2,1)S(1)} all-gather(bf16[128,768]{1,0:T(8,128)(2,1)S(1)} %convolution_convert_fusion.2), channel_id=5, replica_groups=mesh['dp'=8,'head'=4] {'head'}, dimensions={0}, use_global_device_ids=true | all-gather | bytes 983040 | tf_op jit(solution)/shard_map/all_gather | solution.py:40
  591.3 22.2 %reduce-scatter.28.cloned.1.call-done = f32[96,192]{1,0:T(8,128)} async-done(((f32[768,192]{1,0:T(8,128)}), f32[96,192]{1,0:T(8,128)}) %reduce-scatter.28.cloned.1.call-update) | async-done | bytes 73744
  615.2 65.5 %reduce-scatter.30.cloned.1.call-done = f32[96,384]{1,0:T(8,128)} async-done(((f32[768,384]{1,0:T(8,128)}), f32[96,384]{1,0:T(8,128)}) %reduce-scatter.30.cloned.1.call-update) | async-done | bytes 147472
  682.6 68.3 %reduce-scatter.34.cloned.1.call-done = f32[96,576]{1,0:T(8,128)} async-done(((f32[768,576]{1,0:T(8,128)}), f32[96,576]{1,0:T(8,128)}) %reduce-scatter.34.cloned.1.call-update) | async-done | bytes 221200
  752.9 17.2 %copy.62 = bf16[1,4,1578,2,192]{2,4,1,3,0:T(8,128)(2,1)} copy(bf16[1,4,1578,2,192]{4,3,2,1,0:T(2,128)(2,1)} %bitcast.49) | data formatting | bytes 9695232 | tf_op jit(solution)/shard_map/all_to_all | solution.py:279
  775.7 9.0 fusion.13
  794.1 37.8 %all-reduce.1 = (f32[2,2,192]{2,1,0:T(2,128)}, f32[2,768]{1,0:T(2,128)}, f32[2,2,192]{2,1,0:T(2,128)}, f32[5,192]{1,0:T(8,128)}, f32[5,192]{1,0:T(8,128)}) all-reduce(f32[2,2,192]{2,1,0:T(2,128)S(1)} %pad_maximum_fusion.2, f32[2,768]{1,0:T(2,128)S(1)} %pad_maximum_fusion.1, ...), channel_id=1, replica_groups=mesh['dp'=8,'head'=4] {'dp'}, use_global_device_ids=true, to_apply=%region_47.48 | all-reduce | flops 4992 | bytes 39936 | tf_op jit(solution)/shard_map/psum | solution.py:310
  837.1 12.4 %reduce-scatter.24.cloned.1.call-done = f32[96,768]{1,0:T(8,128)} async-done(((f32[768,768]{1,0:T(8,128)}), f32[96,768]{1,0:T(8,128)}) %reduce-scatter.24.cloned.1.call-update) | async-done | bytes 294928 | tf_op jit(solution)/shard_map/reduce_scatter | solution.py:321
  849.5 72.9 %reduce-scatter.26.cloned.1.call-done = f32[768,96]{0,1:T(8,128)} async-done(((f32[768,768]{0,1:T(8,128)}), f32[768,96]{0,1:T(8,128)}) %reduce-scatter.26.cloned.1.call-update) | async-done | bytes 294928 | tf_op jit(solution)/shard_map/reduce_scatter | solution.py:322
  922.5 72.7 %reduce-scatter.20.cloned.1.call-done = f32[96,768]{1,0:T(8,128)} async-done(((f32[768,768]{1,0:T(8,128)}), f32[96,768]{1,0:T(8,128)}) %reduce-scatter.20.cloned.1.call-update) | async-done | bytes 294928 | tf_op jit(solution)/shard_map/reduce_scatter | solution.py:317
  995.2 72.8 %reduce-scatter.22.cloned.1.call-done = f32[768,96]{0,1:T(8,128)} async-done(((f32[768,768]{0,1:T(8,128)}), f32[768,96]{0,1:T(8,128)}) %reduce-scatter.22.cloned.1.call-update) | async-done | bytes 294928 | tf_op jit(solution)/shard_map/reduce_scatter | solution.py:318
  (386 shorter events, 186.9 us)
Async XLA Ops:
  7.2 309.5 %copy-start = (bf16[768,768]{1,0:T(8,128)(2,1)S(1)}, bf16[768,768]{1,0:T(8,128)(2,1)}, u32[]{:S(2)}) copy-start(bf16[768,768]{1,0:T(8,128)(2,1)} %param.31) | copy-start | bytes 3538948
  7.3 144.2 %all-gather.7.cloned.1.call-start = ((), (), s32[]{:S(2)}) async-start(), calls=%async_computation.10 | async-start | bytes 24238080 | tf_op jit(solution)/shard_map/all_gather | solution.py:148
  25.7 206.4 %all-reduce.8.cloned.1.call-start = ((), (), s32[]{:S(2)}) async-start(), calls=%async_computation.11 | async-start | bytes 393216 | tf_op jit(solution)/shard_map/psum | solution.py:36
  26.6 167.4 %copy-start.93 = (f32[3,64]{1,0:T(4,128)}, f32[3,64]{1,0:T(4,128)S(1)}, u32[]{:S(2)}) copy-start(f32[3,64]{1,0:T(4,128)S(1)} %add.336) | copy-start | bytes 2308
  27.3 131.6 %copy-start.46 = (f32[768]{0:T(1024)}, f32[768]{0:T(1024)S(1)}, u32[]{:S(2)}) copy-start(f32[768]{0:T(1024)S(1)} %get-tuple-element.128) | copy-start | bytes 9220
  27.4 145.8 %copy-start.49 = (f32[768]{0:T(1024)}, f32[768]{0:T(1024)S(1)}, u32[]{:S(2)}) copy-start(f32[768]{0:T(1024)S(1)} %get-tuple-element.129) | copy-start | bytes 9220
  28.0 206.5 %copy-start.51 = (f32[768]{0:T(1024)}, f32[768]{0:T(1024)S(1)}, u32[]{:S(2)}) copy-start(f32[768]{0:T(1024)S(1)} %get-tuple-element.132) | copy-start | bytes 9220
  28.0 244.6 %copy-start.54 = (f32[768]{0:T(1024)}, f32[768]{0:T(1024)S(1)}, u32[]{:S(2)}) copy-start(f32[768]{0:T(1024)S(1)} %get-tuple-element.146) | copy-start | bytes 9220
  28.7 154.9 %copy-start.39 = (bf16[128,192]{0,1:T(8,128)(2,1)}, bf16[128,192]{0,1:T(8,128)(2,1)S(1)}, u32[]{:S(2)}) copy-start(bf16[128,192]{0,1:T(8,128)(2,1)S(1)} %fusion.29) | copy-start | bytes 147460
  200.0 71.2 %all-reduce.10.cloned.1.call-start = ((), (), s32[]{:S(2)}) async-start(), calls=%async_computation.12 | async-start | bytes 393216 | tf_op jit(solution)/shard_map/psum | solution.py:36
  239.0 74.1 %all-reduce.12.cloned.1.call-start = ((), (), s32[]{:S(2)}) async-start(), calls=%async_computation.13 | async-start | bytes 393216 | tf_op jit(solution)/shard_map/psum | solution.py:36
  280.9 83.9 %all-reduce.14.cloned.1.call-start = ((), (), s32[]{:S(2)}) async-start(), calls=%async_computation.14 | async-start | bytes 393216 | tf_op jit(solution)/shard_map/psum | solution.py:36
  331.2 256.8 %reduce-scatter.32.cloned.1.call-start = ((), (), s32[]{:S(2)}) async-start(), calls=%async_computation.22 | async-start | bytes 884736
  417.9 171.8 %reduce-scatter.36.cloned.1.call-start = ((), (), s32[]{:S(2)}) async-start(), calls=%async_computation.24 | async-start | bytes 884736
  434.8 178.7 %reduce-scatter.28.cloned.1.call-start = ((), (), s32[]{:S(2)}) async-start(), calls=%async_computation.20 | async-start | bytes 884736
  441.8 238.9 %reduce-scatter.30.cloned.1.call-start = ((), (), s32[]{:S(2)}) async-start(), calls=%async_computation.21 | async-start | bytes 1327104
  463.4 287.5 %reduce-scatter.34.cloned.1.call-start = ((), (), s32[]{:S(2)}) async-start(), calls=%async_computation.23 | async-start | bytes 2211840
  474.1 301.6 %all-gather.9.cloned.1.call-start = ((), (), s32[]{:S(2)}) async-start(), calls=%async_computation.15 | async-start | bytes 2949120 | tf_op jit(solution)/shard_map/all_gather | solution.py:149
  474.9 374.6 %reduce-scatter.24.cloned.1.call-start = ((), (), s32[]{:S(2)}) async-start(), calls=%async_computation.18 | async-start | bytes 2654208 | tf_op jit(solution)/shard_map/reduce_scatter | solution.py:321
  477.0 445.5 %reduce-scatter.26.cloned.1.call-start = ((), (), s32[]{:S(2)}) async-start(), calls=%async_computation.19 | async-start | bytes 2654208 | tf_op jit(solution)/shard_map/reduce_scatter | solution.py:322
  479.0 516.2 %reduce-scatter.20.cloned.1.call-start = ((), (), s32[]{:S(2)}) async-start(), calls=%async_computation.16 | async-start | bytes 2654208 | tf_op jit(solution)/shard_map/reduce_scatter | solution.py:317
  502.7 250.2 %all-to-all-start = ((bf16[1,6312,2,192]{3,2,0,1:T(2,128)(2,1)}), bf16[1,6312,2,192]{3,2,0,1:T(2,128)(2,1)}, u32[]{:S(2)}, u32[]{:S(2)}) async-start(bf16[1,6312,2,192]{3,2,0,1:T(2,128)(2,1)} %copy.61), calls=%async_computation | async-start | bytes 12926976 | tf_op jit(solution)/shard_map/all_to_all | solution.py:279
  508.2 559.8 %reduce-scatter.22.cloned.1.call-start = ((), (), s32[]{:S(2)}) async-start(), calls=%async_computation.17 | async-start | bytes 2654208 | tf_op jit(solution)/shard_map/reduce_scatter | solution.py:318
  831.9 236.1 %copy-start.1 = (bf16[768,768]{1,0:T(8,128)(2,1)S(1)}, bf16[768,768]{1,0:T(8,128)(2,1)}, u32[]{:S(2)}) copy-start(bf16[768,768]{1,0:T(8,128)(2,1)} %param.31) | copy-start | bytes 3538948
  (94 other events, 2476.8 us)
Sparse Core Ops, SparseCore 0:
  25.9 125.5 all-gather.6
  200.1 31.9 all-reduce.7
  239.1 32.0 all-reduce.9
  281.0 32.0 all-reduce.11
  331.4 33.3 all-reduce.13
  418.1 64.2 reduce-scatter.31
  485.7 62.1 reduce-scatter.35
  551.1 62.3 reduce-scatter.27
  616.9 63.7 reduce-scatter.29
  684.6 66.3 reduce-scatter.33
  752.5 23.2 all-gather.8
  779.7 69.8 reduce-scatter.23
  853.6 68.8 reduce-scatter.25
  926.4 68.7 reduce-scatter.19
  999.1 68.8 reduce-scatter.21
